TPU v7x, 128 devices: a whole 4x4x4 slice. The times are simulated.
128 devices in a mesh: vocab: 32 (over x, z, core), group: 4 (over y).
Axes of the slice: x: 4, y: 4, z: 4, core: 2. Of those that a mesh axis runs over, the one named last changes fastest.
Arguments:
- hidden_states: bfloat16 [2048, 4096], P(('group', 'vocab')), parts along dimension 0, may hold values from -32 to 32
- head_weight: bfloat16 [4096, 77824], P(None, 'vocab'), may hold values from -1 to 1
- pick_index: int32 [2048, 64], P('group'), parts along dimension 0, may hold values from 0 to 77823, as said below
- owner_order: int32 [2048], P('group'), parts along dimension 0, may hold values from 0 to 511, each once
Outputs:
- token_logprobs: float32 [2048, 64], P(('group', 'vocab')), parts along dimension 0
- token_logtotal: float32 [2048], P(('group', 'vocab')), parts along dimension 0
There are 4 independent parts, one for each index of `group`. A program takes and returns all parts, laid end to end along the dimension named above; an argument that names none is the same for every part. Nothing has to cross between parts.
Inputs may be any that keep to these rules, and one draw needn't show every extreme that they name: `pick_index`: each row holds 64 distinct vocabulary entries. `owner_order`: each token appears once.
All inputs are finite; a program needn't handle non-finite values.
Results may differ from a plain program's by a relative error of at most 0.0003.
Values may be sent and summed in bfloat16 or wider, within the bound.
No kernel may reach another device: no remote copies, remote signals or barrier semaphores. Data moves between devices by JAX's collectives and lax.ppermute only.
A program may use at most 128 MiB of HBM per device.

v0:
```python
import math

import jax
import jax.numpy as jnp
from jax import lax
from jax.sharding import PartitionSpec as P


def sent_together(arrays, axis, split_dim, concat_dim, along):
    widths = [math.prod(a.shape[along:]) for a in arrays]
    both = jnp.concatenate(
        [a.reshape(*a.shape[:along], w) for a, w in zip(arrays, widths)], axis=along
    )
    filled = lax.all_to_all(both, axis, split_axis=split_dim, concat_axis=concat_dim, tiled=True)
    tiles = jnp.split(filled, [sum(widths[:k]) for k in range(1, len(widths))], axis=along)
    return tuple(
        (b.reshape(*filled.shape[:along], *a.shape[along:]) for a, b in zip(arrays, tiles))
    )


def select_block(pair):
    block_logits, block_index = pair
    columns = lax.broadcasted_iota(jnp.int32, (1, 1, block_logits.shape[1]), 2)
    matches = block_index[:, :, None] == columns
    return jnp.sum(jnp.where(matches, block_logits[:, None, :], 0.0), axis=2)


def local(hidden_states, head_weight, pick_index, owner_order):
    shard_count = lax.axis_size("vocab")
    shard_width = head_weight.shape[1]
    shard_index = lax.axis_index("vocab")
    shard_start = shard_index * shard_width
    own_rows = hidden_states.shape[0]
    pick_count = pick_index.shape[1]
    all_rows = pick_index.shape[0]
    logits = jnp.dot(
        lax.all_gather(hidden_states, "vocab", axis=0, tiled=True),
        head_weight,
        preferred_element_type=jnp.float32,
    )
    local_index = pick_index - shard_start
    block_size = math.gcd(all_rows, 32)
    block_count = all_rows // block_size
    picked = lax.map(
        select_block,
        (
            logits.reshape(block_count, block_size, shard_width),
            local_index.reshape(block_count, block_size, pick_count),
        ),
    )
    picked = picked.reshape(all_rows, pick_count)
    picked = jnp.take(picked, owner_order, axis=0)
    local_max = jnp.max(logits, axis=1)
    local_sum = jnp.sum(jnp.exp(logits - local_max[:, None]), axis=1)
    sent_max = jnp.take(local_max, owner_order, axis=0).reshape(shard_count, own_rows)
    sent_sum = jnp.take(local_sum, owner_order, axis=0).reshape(shard_count, own_rows)
    sent_picks = picked.reshape(shard_count, own_rows, pick_count)
    received_picks, maxima, totals = sent_together(
        (sent_picks, sent_max, sent_sum), "vocab", 0, 0, 2
    )
    overall_max = jnp.max(maxima, axis=0)
    log_total = overall_max + jnp.log(
        jnp.sum(totals * jnp.exp(maxima - overall_max[None, :]), axis=0)
    )
    logprobs = jnp.sum(received_picks, axis=0) - log_total[:, None]
    return (logprobs, log_total)


def solution(mesh):
    in_specs = (P(("group", "vocab"), None), P(None, "vocab"), P("group", None), P("group"))
    out_specs = (P(("group", "vocab"), None), P(("group", "vocab")))
    return jax.shard_map(local, mesh=mesh, in_specs=in_specs, out_specs=out_specs, check_vma=False)
```

profile of v0, /device:TPU:1, one launch (start us, length us, event | category | flops | bytes accessed | tf_op | source)
XLA Modules:
  0.0 171.2 jit_solution(4934463878502503390)
XLA Ops:
  7.2 0.7 all-gather.2.cloned.1.call-update
  7.9 0.9 broadcast_subtract_fusion
  9.0 0.7 compare_select_fusion
  9.7 50.4 %all-gather.2.cloned.1.call-done = bf16[512,4096]{1,0:T(8,128)(2,1)} async-done(((bf16[16,4096]{1,0:T(8,128)(2,1)}), bf16[512,4096]{1,0:T(8,128)(2,1)}) %all-gather.2.cloned.1.call-update) | async-done | bytes 4194320 | tf_op jit(solution)/shard_map/all_gather | solution.py:37
  60.0 16.3 %fusion.4 = (f32[512]{0:T(512)S(1)}, f32[512,2432]{1,0:T(8,128)S(1)}) fusion(bf16[512,4096]{1,0:T(8,128)(2,1)} %all-gather.2.cloned.1.call-done, bf16[4096,2432]{1,0:T(8,128)(2,1)} %param.9), kind=kOutput, calls=%fused_computation.26 | convolution fusion | flops 10201792512 | bytes 29100032 | tf_op jit(solution)/shard_map/dot_general | solution.py:36
  76.4 2.2 %copy-done = f32[512,2432]{1,0:T(8,128)} copy-done((f32[512,2432]{1,0:T(8,128)}, f32[512,2432]{1,0:T(8,128)S(1)}, u32[]{:S(2)}) %copy-start) | copy-done | bytes 4980760
  78.5 0.8 exponential_reduce_fusion
  79.3 3.5 %gather_fusion.1 = f32[512]{0:T(512)S(1)} fusion(f32[512]{0:T(512)S(1)} %get-tuple-element.43, s32[1024]{0:T(1024)S(1)} %pad_clamp_fusion), kind=kCustom, calls=%fused_computation.clone | custom fusion | bytes 6144 | tf_op jit(solution)/shard_map/jit(_take)/gather | solution.py:55
  82.8 3.5 %gather_fusion.2 = f32[512]{0:T(512)S(1)} fusion(f32[512]{0:T(512)S(1)} %exponential_reduce_fusion, s32[1024]{0:T(1024)S(1)} %pad_clamp_fusion), kind=kCustom, calls=%fused_computation.1.clone | custom fusion | bytes 6144 | tf_op jit(solution)/shard_map/jit(_take)/gather | solution.py:56
  86.5 0.2 reshape_reshape.9
  86.7 60.4 %while.10 = (s32[]{:T(128)}, f32[16,32,64]{2,1,0:T(8,128)S(1)}, s32[16,32,64]{2,1,0:T(8,128)S(1)}, f32[16,32,2432]{2,1,0:T(8,128)}, s32[]{:T(128)}) while((s32[]{:T(128)}, f32[16,32,64]{2,1,0:T(8,128)S(1)}, s32[16,32,64]{2,1,0:T(8,128)S(1)}, f32[16,32,2432]{2,1,0:T(8,128)}, s32[]{:T(128)}) %tuple.35), condition=%wide.region_2.3_spmd, body=%wide.region_0.2_spmd.sunk | while | flops 14940162 | bytes 999497 | solution.py:44
  86.7 1.0 dynamic-slice_bitcast_fusion.4
  87.7 2.7 %select_reduce_fusion.2 = f32[32,64]{1,0:T(8,128)S(1)} fusion(f32[32,2432]{1,0:T(8,128)S(1)} %dynamic-slice_bitcast_fusion.4, s32[32,64]{1,0:T(8,128)S(1)} %dynamic-slice_bitcast_fusion.5), kind=kLoop, calls=%fused_computation.3.clone.1 | loop fusion | flops 14940160 | bytes 327680 | tf_op jit(solution)/shard_map/while/body/eval_jaxpr/reduce_sum | solution.py:25
  90.5 1.0 dynamic-slice_bitcast_fusion.4
  91.5 2.7 %select_reduce_fusion.2 = f32[32,64]{1,0:T(8,128)S(1)} fusion(f32[32,2432]{1,0:T(8,128)S(1)} %dynamic-slice_bitcast_fusion.4, s32[32,64]{1,0:T(8,128)S(1)} %dynamic-slice_bitcast_fusion.5), kind=kLoop, calls=%fused_computation.3.clone.1 | loop fusion | flops 14940160 | bytes 327680 | tf_op jit(solution)/shard_map/while/body/eval_jaxpr/reduce_sum | solution.py:25
  94.2 1.0 dynamic-slice_bitcast_fusion.4
  95.2 2.7 %select_reduce_fusion.2 = f32[32,64]{1,0:T(8,128)S(1)} fusion(f32[32,2432]{1,0:T(8,128)S(1)} %dynamic-slice_bitcast_fusion.4, s32[32,64]{1,0:T(8,128)S(1)} %dynamic-slice_bitcast_fusion.5), kind=kLoop, calls=%fused_computation.3.clone.1 | loop fusion | flops 14940160 | bytes 327680 | tf_op jit(solution)/shard_map/while/body/eval_jaxpr/reduce_sum | solution.py:25
  98.0 1.0 dynamic-slice_bitcast_fusion.4
  99.0 2.7 %select_reduce_fusion.2 = f32[32,64]{1,0:T(8,128)S(1)} fusion(f32[32,2432]{1,0:T(8,128)S(1)} %dynamic-slice_bitcast_fusion.4, s32[32,64]{1,0:T(8,128)S(1)} %dynamic-slice_bitcast_fusion.5), kind=kLoop, calls=%fused_computation.3.clone.1 | loop fusion | flops 14940160 | bytes 327680 | tf_op jit(solution)/shard_map/while/body/eval_jaxpr/reduce_sum | solution.py:25
  101.8 1.0 dynamic-slice_bitcast_fusion.4
  102.8 2.7 %select_reduce_fusion.2 = f32[32,64]{1,0:T(8,128)S(1)} fusion(f32[32,2432]{1,0:T(8,128)S(1)} %dynamic-slice_bitcast_fusion.4, s32[32,64]{1,0:T(8,128)S(1)} %dynamic-slice_bitcast_fusion.5), kind=kLoop, calls=%fused_computation.3.clone.1 | loop fusion | flops 14940160 | bytes 327680 | tf_op jit(solution)/shard_map/while/body/eval_jaxpr/reduce_sum | solution.py:25
  105.6 1.0 dynamic-slice_bitcast_fusion.4
  106.6 2.7 %select_reduce_fusion.2 = f32[32,64]{1,0:T(8,128)S(1)} fusion(f32[32,2432]{1,0:T(8,128)S(1)} %dynamic-slice_bitcast_fusion.4, s32[32,64]{1,0:T(8,128)S(1)} %dynamic-slice_bitcast_fusion.5), kind=kLoop, calls=%fused_computation.3.clone.1 | loop fusion | flops 14940160 | bytes 327680 | tf_op jit(solution)/shard_map/while/body/eval_jaxpr/reduce_sum | solution.py:25
  109.3 1.0 dynamic-slice_bitcast_fusion.4
  110.3 2.7 %select_reduce_fusion.2 = f32[32,64]{1,0:T(8,128)S(1)} fusion(f32[32,2432]{1,0:T(8,128)S(1)} %dynamic-slice_bitcast_fusion.4, s32[32,64]{1,0:T(8,128)S(1)} %dynamic-slice_bitcast_fusion.5), kind=kLoop, calls=%fused_computation.3.clone.1 | loop fusion | flops 14940160 | bytes 327680 | tf_op jit(solution)/shard_map/while/body/eval_jaxpr/reduce_sum | solution.py:25
  113.1 1.0 dynamic-slice_bitcast_fusion.4
  114.1 2.7 %select_reduce_fusion.2 = f32[32,64]{1,0:T(8,128)S(1)} fusion(f32[32,2432]{1,0:T(8,128)S(1)} %dynamic-slice_bitcast_fusion.4, s32[32,64]{1,0:T(8,128)S(1)} %dynamic-slice_bitcast_fusion.5), kind=kLoop, calls=%fused_computation.3.clone.1 | loop fusion | flops 14940160 | bytes 327680 | tf_op jit(solution)/shard_map/while/body/eval_jaxpr/reduce_sum | solution.py:25
  116.9 1.0 dynamic-slice_bitcast_fusion.4
  117.9 2.7 %select_reduce_fusion.2 = f32[32,64]{1,0:T(8,128)S(1)} fusion(f32[32,2432]{1,0:T(8,128)S(1)} %dynamic-slice_bitcast_fusion.4, s32[32,64]{1,0:T(8,128)S(1)} %dynamic-slice_bitcast_fusion.5), kind=kLoop, calls=%fused_computation.3.clone.1 | loop fusion | flops 14940160 | bytes 327680 | tf_op jit(solution)/shard_map/while/body/eval_jaxpr/reduce_sum | solution.py:25
  120.6 1.0 dynamic-slice_bitcast_fusion.4
  121.7 2.7 %select_reduce_fusion.2 = f32[32,64]{1,0:T(8,128)S(1)} fusion(f32[32,2432]{1,0:T(8,128)S(1)} %dynamic-slice_bitcast_fusion.4, s32[32,64]{1,0:T(8,128)S(1)} %dynamic-slice_bitcast_fusion.5), kind=kLoop, calls=%fused_computation.3.clone.1 | loop fusion | flops 14940160 | bytes 327680 | tf_op jit(solution)/shard_map/while/body/eval_jaxpr/reduce_sum | solution.py:25
  124.4 1.0 dynamic-slice_bitcast_fusion.4
  125.4 2.7 %select_reduce_fusion.2 = f32[32,64]{1,0:T(8,128)S(1)} fusion(f32[32,2432]{1,0:T(8,128)S(1)} %dynamic-slice_bitcast_fusion.4, s32[32,64]{1,0:T(8,128)S(1)} %dynamic-slice_bitcast_fusion.5), kind=kLoop, calls=%fused_computation.3.clone.1 | loop fusion | flops 14940160 | bytes 327680 | tf_op jit(solution)/shard_map/while/body/eval_jaxpr/reduce_sum | solution.py:25
  128.2 1.0 dynamic-slice_bitcast_fusion.4
  129.2 2.7 %select_reduce_fusion.2 = f32[32,64]{1,0:T(8,128)S(1)} fusion(f32[32,2432]{1,0:T(8,128)S(1)} %dynamic-slice_bitcast_fusion.4, s32[32,64]{1,0:T(8,128)S(1)} %dynamic-slice_bitcast_fusion.5), kind=kLoop, calls=%fused_computation.3.clone.1 | loop fusion | flops 14940160 | bytes 327680 | tf_op jit(solution)/shard_map/while/body/eval_jaxpr/reduce_sum | solution.py:25
  132.0 1.0 dynamic-slice_bitcast_fusion.4
  133.0 2.7 %select_reduce_fusion.2 = f32[32,64]{1,0:T(8,128)S(1)} fusion(f32[32,2432]{1,0:T(8,128)S(1)} %dynamic-slice_bitcast_fusion.4, s32[32,64]{1,0:T(8,128)S(1)} %dynamic-slice_bitcast_fusion.5), kind=kLoop, calls=%fused_computation.3.clone.1 | loop fusion | flops 14940160 | bytes 327680 | tf_op jit(solution)/shard_map/while/body/eval_jaxpr/reduce_sum | solution.py:25
  135.7 1.0 dynamic-slice_bitcast_fusion.4
  136.7 2.7 %select_reduce_fusion.2 = f32[32,64]{1,0:T(8,128)S(1)} fusion(f32[32,2432]{1,0:T(8,128)S(1)} %dynamic-slice_bitcast_fusion.4, s32[32,64]{1,0:T(8,128)S(1)} %dynamic-slice_bitcast_fusion.5), kind=kLoop, calls=%fused_computation.3.clone.1 | loop fusion | flops 14940160 | bytes 327680 | tf_op jit(solution)/shard_map/while/body/eval_jaxpr/reduce_sum | solution.py:25
  139.5 1.0 dynamic-slice_bitcast_fusion.4
  140.5 2.7 %select_reduce_fusion.2 = f32[32,64]{1,0:T(8,128)S(1)} fusion(f32[32,2432]{1,0:T(8,128)S(1)} %dynamic-slice_bitcast_fusion.4, s32[32,64]{1,0:T(8,128)S(1)} %dynamic-slice_bitcast_fusion.5), kind=kLoop, calls=%fused_computation.3.clone.1 | loop fusion | flops 14940160 | bytes 327680 | tf_op jit(solution)/shard_map/while/body/eval_jaxpr/reduce_sum | solution.py:25
  143.3 1.0 dynamic-slice_bitcast_fusion.4
  144.3 2.7 %select_reduce_fusion.2 = f32[32,64]{1,0:T(8,128)S(1)} fusion(f32[32,2432]{1,0:T(8,128)S(1)} %dynamic-slice_bitcast_fusion.4, s32[32,64]{1,0:T(8,128)S(1)} %dynamic-slice_bitcast_fusion.5), kind=kLoop, calls=%fused_computation.3.clone.1 | loop fusion | flops 14940160 | bytes 327680 | tf_op jit(solution)/shard_map/while/body/eval_jaxpr/reduce_sum | solution.py:25
  147.0 1.0 gather_fusion
  148.1 0.2 reshape_reshape.8
  148.6 14.1 %all_to_all.5 = f32[32,16,66]{2,1,0:T(8,128)S(1)} all-to-all(f32[32,16,66]{2,1,0:T(8,128)S(1)} %pad_maximum_fusion), channel_id=1, replica_groups=mesh['vocab'=32,'group'=4] {'vocab'}, dimensions={0} | all-to-all | bytes 270336 | tf_op jit(solution)/shard_map/all_to_all | solution.py:14
  162.7 0.3 fusion.3
  163.7 0.7 copy.26
  (53 shorter events, 1.6 us)
Async XLA Ops:
  7.2 52.9 %all-gather.2.cloned.1.call-start = ((), (), s32[]{:S(2)}) async-start(), calls=%async_computation.1 | async-start | bytes 4325376 | tf_op jit(solution)/shard_map/all_gather | solution.py:37
  76.3 2.2 %copy-start = (f32[512,2432]{1,0:T(8,128)}, f32[512,2432]{1,0:T(8,128)S(1)}, u32[]{:S(2)}) copy-start(f32[512,2432]{1,0:T(8,128)S(1)} %get-tuple-element.44) | copy-start | bytes 14942212
  76.3 10.0 %copy-start.1 = (s32[512]{0:T(512)S(1)}, s32[512]{0:T(512)}, u32[]{:S(2)}) copy-start(s32[512]{0:T(512)} %param.11) | copy-start | bytes 6148
  163.6 0.8 copy-start.2
Sparse Core Ops, SparseCore 0:
  10.2 49.7 all-gather.1
where the time goes:
time: 172 us; the launch traced here: 171 us
  waiting for transfers between devices  51 us (30%)
  other arithmetic  47.3 us (28%)
  local copies, waits for them, and re-layouts  28.1 us (16%)
  matrix products  16.3 us (9%)
  between operations  14.2 us (8%)
  blocking collectives  14.1 us (8%)
    all_gather x1, waiting for transfers between devices, local(): lax.all_gather(hidden_states, 'vocab', axis=0, tiled=True)  50.4 us
    reduce_sum x16, other arithmetic, select_block(): return jnp.sum(jnp.where(matches, block_logits[:, None, :], 0.0), axis=2)  44 us
    dot_general x1, matrix products, local(): jnp.dot(lax.all_gather(hidden_states, 'vocab', axis=0, tiled=True), head_...  16.3 us
    broadcast_in_dim x16, local copies, waits for them, and re-layouts, select_block(): return jnp.sum(jnp.where(matches, block_logits[:, None, :], 0.0), axis=2)  15.9 us
    all_to_all x1, blocking collectives, sent_together(): lax.all_to_all(both, axis, split_axis=split_dim, concat_axis=concat_dim,...  14.1 us
    gather x1, local copies, waits for them, and re-layouts, local(): jnp.take(local_sum, owner_order, axis=0).reshape(shard_count, own_rows)  3.49 us
    gather x1, local copies, waits for them, and re-layouts, local(): jnp.take(local_max, owner_order, axis=0).reshape(shard_count, own_rows)  3.49 us
  transfers between devices with their start and end apart: 1, of which 1 were waited for; matrix products, arithmetic and copies ran while one was open for 1% of the time, Pallas kernels for 0%

commit v1 on v0

v1 whole, which is shorter than its diff:
```python
import functools

import jax
import jax.numpy as jnp
from jax import lax
from jax.experimental import pallas as pl
from jax.experimental.pallas import tpu as pltpu
from jax.sharding import PartitionSpec as P

LANES = 128
ROWS = 8


def pick_kernel(order_ref, logits_ref, index_ref, out_ref, held_ref, *, unroll):
    tokens, width = logits_ref.shape
    picks = index_ref.shape[1]
    lane = lax.broadcasted_iota(jnp.int32, (ROWS, LANES), 1)

    def block(b, _):
        rows = pl.ds(pl.multiple_of(b * ROWS, ROWS), ROWS)
        local = index_ref[rows, :]
        tile = lax.shift_right_arithmetic(local, 7)
        at = lax.bitwise_and(local, LANES - 1)
        top = jnp.max(logits_ref[rows, :], axis=1, keepdims=True)
        total = jnp.sum(jnp.exp(logits_ref[rows, :] - top), axis=1, keepdims=True)
        found = jnp.zeros((ROWS, LANES), jnp.float32)
        for j in range(width // LANES):
            part = logits_ref[rows, j * LANES : (j + 1) * LANES]
            seen = jnp.take_along_axis(part, at, axis=1, mode="promise_in_bounds")
            found = jnp.where(tile == j, seen, found)
        found = jnp.where(lane == LANES - 2, top, found)
        found = jnp.where(lane == LANES - 1, total, found)
        held_ref[rows, :] = found
        return 0

    lax.fori_loop(0, tokens // ROWS, block, 0)

    def move(b, _):
        for i in range(unroll):
            r = b * unroll + i
            out_ref[pl.ds(r, 1), :] = held_ref[pl.ds(order_ref[r], 1), :]
        return 0

    lax.fori_loop(0, tokens // unroll, move, 0)


def picked_and_stats(logits, local_index, owner_order):
    tokens, width = logits.shape
    spare = LANES - local_index.shape[1]
    index = jnp.pad(local_index, ((0, 0), (0, spare)), constant_values=-1)
    return pl.pallas_call(
        functools.partial(pick_kernel, unroll=16),
        out_shape=jax.ShapeDtypeStruct((tokens, LANES), jnp.float32),
        in_specs=[
            pl.BlockSpec(memory_space=pltpu.SMEM),
            pl.BlockSpec(memory_space=pltpu.VMEM),
            pl.BlockSpec(memory_space=pltpu.VMEM),
        ],
        out_specs=pl.BlockSpec(memory_space=pltpu.VMEM),
        scratch_shapes=[pltpu.VMEM((tokens, LANES), jnp.float32)],
        compiler_params=pltpu.CompilerParams(vmem_limit_bytes=24 * 1024 * 1024),
        cost_estimate=pl.CostEstimate(
            flops=4 * tokens * width,
            bytes_accessed=4 * tokens * width,
            transcendentals=tokens * width,
        ),
    )(owner_order, logits, index)


def local(hidden_states, head_weight, pick_index, owner_order):
    shard_count = lax.axis_size("vocab")
    shard_start = lax.axis_index("vocab") * head_weight.shape[1]
    own_rows = hidden_states.shape[0]
    pick_count = pick_index.shape[1]
    logits = jnp.dot(
        lax.all_gather(hidden_states, "vocab", axis=0, tiled=True),
        head_weight,
        preferred_element_type=jnp.float32,
    )
    rows = picked_and_stats(logits, pick_index - shard_start, owner_order)
    rows = rows.reshape(shard_count, own_rows, LANES)
    received = lax.all_to_all(rows, "vocab", split_axis=0, concat_axis=0, tiled=True)
    maxima = received[:, :, LANES - 2]
    totals = received[:, :, LANES - 1]
    overall_max = jnp.max(maxima, axis=0)
    log_total = overall_max + jnp.log(
        jnp.sum(totals * jnp.exp(maxima - overall_max[None, :]), axis=0)
    )
    logprobs = jnp.sum(received[:, :, :pick_count], axis=0) - log_total[:, None]
    return (logprobs, log_total)


def solution(mesh):
    in_specs = (P(("group", "vocab"), None), P(None, "vocab"), P("group", None), P("group"))
    out_specs = (P(("group", "vocab"), None), P(("group", "vocab")))
    return jax.shard_map(local, mesh=mesh, in_specs=in_specs, out_specs=out_specs, check_vma=False)
```

time: 172 us -> 113 us (0.66)
  other arithmetic: 47.3 us -> 0.54 us
  local copies, waits for them, and re-layouts: 28.1 us -> 2.22 us
  Pallas kernels: 0 us -> 14.1 us
    reduce_sum x18 -> x1, other arithmetic: 44.8 us -> 0.04 us  [local(): logprobs = jnp.sum(received[:, :, :pick_count], axis=0) - log_total[:, None]]
    broadcast_in_dim x17 -> x0, local copies, waits for them, and re-layouts: 16 us -> none  [the longest x16 15.9 us: select_block(): return jnp.sum(jnp.where(matches, block_logits[:, None, :], 0.0), axis=2)]
    pallas_call x0 -> x1, Pallas kernels: none -> 14.1 us  [picked_and_stats(): pl.pallas_call(functools.partial(pick_kernel, unroll=16), out_shape=jax.S...]
    gather x3 -> x0, local copies, waits for them, and re-layouts: 8.01 us -> none  [the longest x1 3.49 us: local(): jnp.take(local_sum, owner_order, axis=0).reshape(shard_count, own_rows)]
where the time goes in v1:
time: 113 us
  waiting for transfers between devices  51.7 us (46%)
  matrix products  15.9 us (14%)
  Pallas kernels  14.1 us (12%)
  blocking collectives  14.1 us (12%)
  between operations  14.1 us (12%)
  local copies, waits for them, and re-layouts  2.22 us (2%)
    all_gather x1, waiting for transfers between devices, local(): lax.all_gather(hidden_states, 'vocab', axis=0, tiled=True)  51 us
    dot_general x1, matrix products, local(): jnp.dot(lax.all_gather(hidden_states, 'vocab', axis=0, tiled=True), head_...  15.9 us
    pallas_call x1, Pallas kernels, picked_and_stats(): pl.pallas_call(functools.partial(pick_kernel, unroll=16), out_shape=jax.S...  14.1 us
    all_to_all x1, blocking collectives, local(): lax.all_to_all(rows, 'vocab', split_axis=0, concat_axis=0, tiled=True)  14.1 us
  transfers between devices with their start and end apart: 1, of which 1 were waited for; matrix products, arithmetic and copies ran while one was open for 1% of the time, Pallas kernels for 0%

profile of v1, /device:TPU:1, one launch (start us, length us, event | category | flops | bytes accessed | tf_op | source)
XLA Modules:
  0.0 112.6 jit_solution(17558274922096759716)
XLA Ops:
  7.2 0.0 all-gather.2.cloned.1.call-start
  7.2 0.7 all-gather.2.cloned.1.call-update
  7.9 1.0 copy.15
  9.0 0.0 copy-start
  9.0 51.0 %all-gather.2.cloned.1.call-done = bf16[512,4096]{1,0:T(8,128)(2,1)} async-done(((bf16[16,4096]{1,0:T(8,128)(2,1)}), bf16[512,4096]{1,0:T(8,128)(2,1)}) %all-gather.2.cloned.1.call-update) | async-done | bytes 4194320 | tf_op jit(solution)/shard_map/all_gather | solution.py:76
  60.0 15.9 %fusion.4.logits_ref = f32[512,2432]{1,0:T(8,128)S(1)} fusion(bf16[512,4096]{1,0:T(8,128)(2,1)} %all-gather.2.cloned.1.call-done, bf16[4096,2432]{1,0:T(8,128)(2,1)} %param.5), kind=kOutput, calls=%fused_computation.10 | convolution fusion | flops 10200547328 | bytes 29097984 | tf_op jit(solution)/shard_map/dot_general | solution.py:75
  75.9 0.0 copy-done
  75.9 14.1 %shard_map.59 = f32[512,128]{1,0:T(8,128)S(1)} custom-call(s32[512]{0:T(512)S(1)} %copy-done, f32[512,2432]{1,0:T(8,128)S(1)} %fusion.4.logits_ref, s32[512,128]{1,0:T(8,128)S(1)} %pad.4.index_ref), custom_call_target="tpu_custom_call" | custom-call | flops 4980736 | bytes 4980736 | tf_op jit(solution)/shard_map/pallas_call | solution.py:51
  90.0 14.1 %all_to_all.5 = f32[32,16,128]{2,1,0:T(8,128)S(1)} all-to-all(f32[32,16,128]{2,1,0:T(8,128)S(1)} %bitcast.13), channel_id=1, replica_groups=mesh['vocab'=32,'group'=4] {'vocab'}, dimensions={0} | all-to-all | bytes 524288 | tf_op jit(solution)/shard_map/all_to_all | solution.py:82
  104.1 0.3 fusion.3
  104.4 0.2 copy.22
  104.6 0.2 copy.23
  104.8 0.2 fusion.2
  105.0 0.0 copy-start.1
  105.0 0.1 copy.21
  105.1 0.7 copy.20
  105.8 0.0 copy-done.1
  (5 shorter events, 0.1 us)
Async XLA Ops:
  7.2 52.9 %all-gather.2.cloned.1.call-start = ((), (), s32[]{:S(2)}) async-start(), calls=%async_computation.1 | async-start | bytes 4325376 | tf_op jit(solution)/shard_map/all_gather | solution.py:76
  9.0 66.9 %copy-start = (s32[512]{0:T(512)S(1)}, s32[512]{0:T(512)}, u32[]{:S(2)}) copy-start(s32[512]{0:T(512)} %order_ref.1) | copy-start | bytes 6148
  105.0 0.8 copy-start.1
Sparse Core Ops, SparseCore 0:
  10.2 49.7 all-gather.1
